TPU v7x, 32 devices: a whole 2x2x4 slice. The times are simulated.
32 devices in a mesh: seq: 8 (over z, x), head: 4 (over y, core).
Axes of the slice: x: 2, y: 2, z: 4, core: 2. Of those that a mesh axis runs over, the one named last changes fastest.
Arguments:
- query_in: bfloat16 [2048, 8192], P('seq', 'head'), may hold values from -1.796875 to 1.796875
- key_in: bfloat16 [2048, 8192], P('seq', 'head'), may hold values from -1.796875 to 1.796875
- value_in: bfloat16 [2048, 8192], P('seq', 'head'), may hold values from -11 to 11
- log_decay: float32 [2048, 64], P('seq', 'head'), may hold values from -1 to 0, as said below
- norm_gain: float32 [8192], P('head'), may hold values from 0.5 to 1.5
- prompt_lengths: int32 [4], replicated, may hold values from 1 to 1536, 2048 in all
- step_query: bfloat16 [4, 128, 8192], P(None, 'seq', 'head'), may hold values from -1.796875 to 1.796875
- step_key: bfloat16 [4, 128, 8192], P(None, 'seq', 'head'), may hold values from -1.796875 to 1.796875
- step_value: bfloat16 [4, 128, 8192], P(None, 'seq', 'head'), may hold values from -6 to 6
- step_decay: float32 [4, 128, 64], P(None, 'seq', 'head'), may hold values from -0.3 to -0.01
- row_prompt: int32 [128], P('seq'), may hold values from 0 to 3
Outputs:
- attn_out: bfloat16 [2048, 8192], P('seq', 'head')
- decode_out: bfloat16 [4, 128, 8192], P(None, 'seq', 'head')
Inputs may be any that keep to these rules, and one draw needn't show every extreme that they name: `log_decay`: Negative; per head and token.
All inputs are finite; a program needn't handle non-finite values.
Results may differ from a plain program's by a relative error of at most 0.0056.
Values sent between devices are 32-bit elements; how exact they have to be, the bound alone decides.
A program may use at most 64 MiB of HBM per device.

v0:
```python
import functools

import jax
import jax.numpy as jnp
from jax import lax
from jax.experimental import pallas as pl
from jax.experimental.pallas import tpu as pltpu
from jax.sharding import PartitionSpec as P

HEAD_COUNT = 64
HDIM = 128
BLOCK = 256
PROMPTS = 4
PAIR = 2


EPSILON = 1e-06
MESH = pl.DeviceIdType.MESH


def fused_kernel(
    n,
    steps,
    query_ref,
    key_ref,
    value_ref,
    token_ref,
    bias_ref,
    coef_ref,
    mask_ref,
    sq_ref,
    sk_ref,
    sv_ref,
    weight_ref,
    row_ref,
    mixed_ref,
    square_ref,
    dec_ref,
    dsquare_ref,
    own_part,
    x_send,
    x_recv,
    coef_recv,
    q_send,
    q_recv,
    row_recv,
    f_recv,
    f_send,
    b_recv,
    b_send,
    pair_part,
    t_recv,
    t_send,
    e_mine,
    acc_sq,
    acc_dsq,
    e_send,
    e_recv,
    r_send,
    r_recv,
    xs_sem,
    xr_sem,
    cs_sem,
    cr_sem,
    qs_sem,
    qr_sem,
    ws_sem,
    wr_sem,
    fs_sem,
    fr_sem,
    bs_sem,
    br_sem,
    ts_sem,
    tr_sem,
    es_sem,
    er_sem,
    rs_sem,
    rr_sem,
):
    f32, bf16 = jnp.float32, jnp.bfloat16
    me = lax.axis_index("seq")
    side = lax.rem(me, PAIR)
    rank = me // PAIR
    ranks = n // PAIR
    partner = me + 1 - 2 * side
    half, slots = own_part.shape[:2]
    rows = sq_ref.shape[0] // steps
    mine = side * half
    theirs = (1 - side) * half
    is_first = rank == 0
    is_last = rank == ranks - 1
    low = side == 0
    ahead = lax.rem(me + PAIR, n)
    behind = lax.rem(me + n - PAIR, n)

    def copy(src, dst, send, recv, to):
        return pltpu.make_async_remote_copy(
            src_ref=src,
            dst_ref=dst,
            send_sem=send,
            recv_sem=recv,
            device_id={"seq": to},
            device_id_type=MESH,
        )

    def x_copy(j, p):
        i = j * slots + p
        return copy(x_send.at[j, p], x_recv.at[j, p], xs_sem.at[i], xr_sem.at[i], partner)

    def f_copy(j, p):
        i = j * slots + p
        return copy(f_send.at[j, p], f_recv.at[j, p], fs_sem.at[i], fr_sem.at[i], ahead)

    def b_copy(j, p):
        i = j * slots + p
        return copy(b_send.at[j, p], b_recv.at[j, p], bs_sem.at[i], br_sem.at[i], behind)

    def q_copy(j):
        return copy(q_send.at[j], q_recv.at[j], qs_sem.at[j], qr_sem.at[j], partner)

    def e_copy(j):
        return copy(e_send.at[j], e_recv.at[j], es_sem.at[j], er_sem.at[j], partner)

    def r_copy(j):
        return copy(r_send.at[j], r_recv.at[j], rs_sem.at[j], rr_sem.at[j], partner)

    coef_copy = copy(coef_ref.at[pl.ds(theirs, half)], coef_recv, cs_sem, cr_sem, partner)
    row_copy = copy(row_ref, row_recv, ws_sem, wr_sem, partner)

    t_copy = copy(t_send, t_recv, ts_sem, tr_sem, behind)

    def lanes(h):
        return pl.ds(pl.multiple_of(h * HDIM, HDIM), HDIM)

    barrier = pltpu.get_barrier_semaphore()
    pl.semaphore_signal(barrier, inc=1, device_id={"seq": partner}, device_id_type=MESH)

    @pl.when(jnp.logical_not(is_last))
    def _():
        pl.semaphore_signal(barrier, inc=1, device_id={"seq": ahead}, device_id_type=MESH)

    @pl.when(jnp.logical_not(is_first))
    def _():
        pl.semaphore_signal(barrier, inc=1, device_id={"seq": behind}, device_id_type=MESH)

    def make_parts(h, j, into):
        key = key_ref[:, lanes(h)].astype(f32)
        value = value_ref[:, lanes(h)]
        cols = jnp.transpose(token_ref[h])
        for p in range(slots):
            keyed = (key * cols[:, p : p + 1]).astype(bf16)
            into[j, p] = lax.dot_general(
                keyed, value, (((0,), (0,)), ((), ())), preferred_element_type=f32
            )

    def within(h):
        query = query_ref[:, lanes(h)]
        scores = lax.dot_general(
            query, key_ref[:, lanes(h)], (((1,), (1,)), ((), ())), preferred_element_type=f32
        )
        cols = jnp.transpose(token_ref[h])
        spread = cols[:, slots : slots + 1] - token_ref[h, slots : slots + 1, :] + bias_ref[...]
        weights = (scores * jnp.exp(spread)).astype(bf16)
        mixed_ref[:, lanes(h)] = jnp.dot(
            weights, value_ref[:, lanes(h)], preferred_element_type=f32
        )

    def across(h, entry):
        carried = jnp.transpose(token_ref[h])[:, slots + 1 : slots + 2]
        outer = jnp.dot(query_ref[:, lanes(h)], entry.astype(bf16), preferred_element_type=f32)
        mixed = mixed_ref[:, lanes(h)] + outer * carried
        mixed_ref[:, lanes(h)] = mixed
        acc_sq[...] += mixed * mixed

    def own_steps(h):
        query = sq_ref[:, lanes(h)].astype(f32)
        key = sk_ref[:, lanes(h)].astype(f32)
        value = sv_ref[:, lanes(h)].astype(f32)
        weight = weight_ref[h]
        cut = lambda a, i: a[i * rows : (i + 1) * rows]
        spot = 0
        for i in range(steps):
            total = None
            for j in range(i + 1):
                dot = jnp.sum(cut(query, i) * cut(key, j), axis=1, keepdims=True)
                term = dot * weight[:, spot : spot + 1] * cut(value, j)
                total = term if j == 0 else total + term
                spot += 1
            dec_ref[i * rows : (i + 1) * rows, lanes(h)] = total

    def from_state(h, product):
        weight = weight_ref[h]
        spot = steps * (steps + 1) // 2
        for i in range(steps):
            at = slice(i * rows, (i + 1) * rows)
            out = dec_ref[at, lanes(h)] + weight[:, spot + i : spot + i + 1] * product[at]
            dec_ref[at, lanes(h)] = out
            acc_dsq[at] += out * out

    acc_sq[...] = jnp.zeros_like(acc_sq)
    acc_dsq[...] = jnp.zeros_like(acc_dsq)
    make_parts(theirs, 0, x_send)
    pl.semaphore_wait(barrier, 1 + jnp.where(is_first, 0, 1) + jnp.where(is_last, 0, 1))
    coef_copy.start()

    @pl.loop(0, half)
    def _(j):
        @pl.when(j > 0)
        def _():
            make_parts(theirs + j, j, x_send)

        for p in range(slots):
            x_copy(j, p).start()

        @pl.when(j == 0)
        def _():
            row_copy.start()

        q_send[j] = sq_ref[:, lanes(theirs + j)].astype(f32)
        q_copy(j).start()
        make_parts(mine + j, j, own_part)

    @pl.when(is_first)
    def _():
        f_recv[...] = jnp.zeros_like(f_recv)

    @pl.when(is_last)
    def _():
        b_recv[...] = jnp.zeros_like(b_recv)

    coef_copy.wait()
    row_copy.wait()

    @pl.when(is_last)
    def _():
        t_recv[...] = jnp.ones_like(t_recv)

    lag_f = rank
    lag_b = ranks - 1 - rank
    lag_d = jnp.maximum(lag_f, lag_b)

    def relay_decay():
        @pl.when(jnp.logical_not(is_last))
        def _():
            t_copy.wait_recv()

        @pl.when(jnp.logical_not(is_first))
        def _():
            t_send[...] = t_recv[...] * coef_recv[...] * coef_ref[pl.ds(mine, half)]
            t_copy.start()

    def rows_of(j, p):
        c_own = coef_ref[mine + j, pl.ds(p, 1), :]
        c_other = coef_recv[j, pl.ds(p, 1), :]
        return jnp.where(low, c_own, c_other), jnp.where(low, c_other, c_own)

    def combine(j):
        for p in range(slots):
            x_copy(j, p).wait_recv()
            own = own_part[j, p]
            other = x_recv[j, p]
            c_low, c_high = rows_of(j, p)
            pair = c_high * jnp.where(low, own, other) + jnp.where(low, other, own)
            pair_part[j, p] = pair

            @pl.when(is_first)
            def _():
                f_send[j, p] = pair

                @pl.when(jnp.logical_not(is_last))
                def _():
                    f_copy(j, p).start()

            @pl.when(is_last & jnp.logical_not(is_first))
            def _():
                b_send[j, p] = pair
                b_copy(j, p).start()

    def forward(j):
        acc_mine = None
        acc_theirs = None
        for p in range(slots):
            c_low, c_high = rows_of(j, p)

            @pl.when(jnp.logical_not(is_first))
            def _():
                f_copy(j, p).wait_recv()
                f_send[j, p] = (c_low * c_high) * f_recv[j, p] + pair_part[j, p]

                @pl.when(jnp.logical_not(is_last))
                def _():
                    f_copy(j, p).start()

            came = f_recv[j, p]
            middle = c_low * came + jnp.where(low, own_part[j, p], x_recv[j, p])
            at_low = came * mask_ref[pl.ds(p, 1), :]
            at_high = middle * mask_ref[pl.ds(slots + p, 1), :]
            to_mine = jnp.where(low, at_low, at_high)
            to_theirs = jnp.where(low, at_high, at_low)
            acc_mine = to_mine if p == 0 else acc_mine + to_mine
            acc_theirs = to_theirs if p == 0 else acc_theirs + to_theirs
        e_send[j] = acc_theirs
        e_copy(j).start()
        e_mine[j] = acc_mine

    def backward(j):
        for p in range(slots):

            @pl.when(jnp.logical_not(is_last))
            def _():
                b_copy(j, p).wait_recv()

                @pl.when(jnp.logical_not(is_first))
                def _():
                    b_send[j, p] = b_recv[j, p] + t_recv[j, pl.ds(p, 1), :] * pair_part[j, p]
                    b_copy(j, p).start()

    def decode(j):
        q_copy(j).wait_recv()
        q_own = sq_ref[:, lanes(mine + j)]
        q_other = q_recv[j].astype(bf16)
        total_own = None
        total_other = None
        for p in range(slots):
            final = t_recv[j, pl.ds(p, 1), :] * f_send[j, p] + b_recv[j, p]
            final_half = final.astype(bf16)
            got_own = jnp.dot(q_own, final_half, preferred_element_type=f32)
            got_other = jnp.dot(q_other, final_half, preferred_element_type=f32)
            got_own = jnp.where(row_ref[...] == float(p), got_own, 0.0)
            got_other = jnp.where(row_recv[...] == float(p), got_other, 0.0)
            total_own = got_own if p == 0 else total_own + got_own
            total_other = got_other if p == 0 else total_other + got_other
        r_send[j] = total_other
        r_copy(j).start()
        from_state(mine + j, total_own)

    @pl.loop(0, half + ranks - 1)
    def _(t):
        @pl.when(t < half)
        def _():
            own_steps(t)
            own_steps(half + t)
            within(mine + t)
            within(theirs + t)

        @pl.when(t == lag_b)
        def _():
            relay_decay()

        @pl.when(t < half)
        def _():
            combine(t)

        @pl.when((t >= lag_f) & (t < half + lag_f))
        def _():
            forward(t - lag_f)

        @pl.when((t >= lag_b) & (t < half + lag_b))
        def _():
            backward(t - lag_b)

        @pl.when((t >= lag_d) & (t < half + lag_d))
        def _():
            decode(t - lag_d)

        @pl.when((t >= lag_f) & (t < half + lag_f))
        def _():
            across(mine + t - lag_f, e_mine[t - lag_f])

    @pl.loop(0, half)
    def _(j):
        e_copy(j).wait()
        across(theirs + j, e_recv[j])

    @pl.loop(0, half)
    def _(j):
        r_copy(j).wait()
        from_state(theirs + j, r_recv[j])
        q_copy(j).wait_send()
        for p in range(slots):
            x_copy(j, p).wait_send()

            @pl.when(jnp.logical_not(is_last))
            def _():
                f_copy(j, p).wait_send()

            @pl.when(jnp.logical_not(is_first))
            def _():
                b_copy(j, p).wait_send()

    @pl.when(jnp.logical_not(is_first))
    def _():
        t_copy.wait_send()

    def row_sums(acc):
        return lax.dot_general(
            jnp.ones((8, HDIM), f32),
            acc[...],
            (((1,), (1,)), ((), ())),
            precision=lax.Precision.HIGHEST,
            preferred_element_type=f32,
        )

    square_ref[...] = row_sums(acc_sq)
    dsquare_ref[...] = row_sums(acc_dsq)


def fused(n, steps, *operands):
    query, coef, step = operands[0], operands[5], operands[7]
    tok, width = query.shape
    heads, slots = coef.shape[:2]
    half = heads // PAIR
    vectors = step.shape[0]
    chunks = half * slots
    f32 = jnp.float32
    vmem = pl.BlockSpec(memory_space=pltpu.VMEM)
    dma = pltpu.SemaphoreType.DMA
    states = pltpu.VMEM((half, slots, HDIM, HDIM), f32)
    decays = pltpu.VMEM((half,) + coef.shape[1:], f32)
    entries = pltpu.VMEM((half, HDIM, HDIM), f32)
    products = pltpu.VMEM((half, vectors, HDIM), f32)
    return pl.pallas_call(
        functools.partial(fused_kernel, n, steps),
        out_shape=(
            jax.ShapeDtypeStruct((tok, width), f32),
            jax.ShapeDtypeStruct((8, tok), f32),
            jax.ShapeDtypeStruct((vectors, width), f32),
            jax.ShapeDtypeStruct((8, vectors), f32),
        ),
        in_specs=[vmem] * len(operands),
        out_specs=(vmem,) * 4,
        scratch_shapes=[
            states,
            states,
            states,
            decays,
            products,
            products,
            pltpu.VMEM((vectors, HDIM), f32),
            states,
            states,
            states,
            states,
            states,
            decays,
            decays,
            entries,
            pltpu.VMEM((tok, HDIM), f32),
            pltpu.VMEM((vectors, HDIM), f32),
            entries,
            entries,
            products,
            products,
            dma((chunks,)),
            dma((chunks,)),
            dma,
            dma,
            dma((half,)),
            dma((half,)),
            dma,
            dma,
            dma((chunks,)),
            dma((chunks,)),
            dma((chunks,)),
            dma((chunks,)),
            dma,
            dma,
            dma((half,)),
            dma((half,)),
            dma((half,)),
            dma((half,)),
        ],
        compiler_params=pltpu.CompilerParams(
            collective_id=0, has_side_effects=True, vmem_limit_bytes=56 * 1024 * 1024
        ),
        name="fused",
    )(*operands)


def ends_of(prompt_lengths):
    index = jnp.arange(prompt_lengths.shape[0])
    return jnp.sum(jnp.where(index[:, None] >= index[None, :], prompt_lengths[None, :], 0), axis=1)


def segment_ids(prompt_lengths, positions):
    boundary = ends_of(prompt_lengths)
    return jnp.sum((positions[:, None] >= boundary[None, :]).astype(jnp.int32), axis=1)


def local(
    n,
    query_in,
    key_in,
    value_in,
    log_decay,
    norm_gain,
    prompt_lengths,
    step_query,
    step_key,
    step_value,
    step_decay,
    row_prompt,
):
    f32 = jnp.float32
    tok = query_in.shape[0]
    heads = log_decay.shape[1]
    steps, rows = step_query.shape[:2]
    place = lax.axis_index("seq")
    first = place * tok
    pair_first = (place // PAIR) * (PAIR * tok)
    ends = ends_of(prompt_lengths)
    begins = ends - prompt_lengths
    segs = segment_ids(prompt_lengths, first + jnp.arange(tok, dtype=jnp.int32))
    slot = jnp.arange(PROMPTS, dtype=jnp.int32)

    def seg_before(token):
        return jnp.where(token > 0, segment_ids(prompt_lengths, (token - 1)[None])[0], -1)

    seg_front = seg_before(first)
    cum = jnp.cumsum(log_decay, axis=0)

    last = jnp.clip(ends - first, 1, tok) - 1
    reached = jnp.sum(
        jnp.where((jnp.arange(tok)[None, :] == last[:, None])[:, :, None], cum[None], 0.0), axis=1
    )
    taken = (segs[None, :] == slot[:, None])[:, :, None]
    keep = jnp.where(taken, jnp.exp(jnp.where(taken, reached[:, None, :] - cum[None], 0.0)), 0.0)
    carried = jnp.exp(cum) * (segs == seg_front).astype(f32)[:, None]
    spare = jnp.zeros_like(keep[:2])
    tokens = jnp.transpose(jnp.concatenate([keep, cum[None], carried[None], spare]), (2, 0, 1))
    causal = jnp.arange(tok)[:, None] >= jnp.arange(tok)[None, :]
    linked = causal & (segs[:, None] == segs[None, :])
    bias = jnp.where(linked, 0.0, -jnp.inf)
    coef = jnp.where(
        (ends <= first)[:, None], 1.0, jnp.where((begins < first)[:, None], jnp.exp(reached), 0.0)
    )
    coef = jnp.broadcast_to(coef.T[:, :, None], (heads, PROMPTS, HDIM))
    pair_last = pair_first + PAIR * tok
    marks = jnp.concatenate(
        [slot == seg_before(pair_first), slot == seg_before(pair_first + tok), ends <= pair_last]
    )
    marks = jnp.concatenate([marks, jnp.zeros((4,), bool)])
    masks = jnp.broadcast_to(marks.astype(f32)[:, None], (marks.shape[0], HDIM))

    shares = [
        [float(j < k <= i) for k in range(steps)] for i in range(steps) for j in range(i + 1)
    ]
    wholes = [[float(k <= i) for k in range(steps)] for i in range(steps)]
    step_weights = jnp.exp(
        jnp.einsum(
            "irh,wi->hrw", step_decay, jnp.array(shares + wholes, f32), precision=lax.Precision.HIGHEST
        )
    )
    row_marks = jnp.broadcast_to(
        jnp.broadcast_to(row_prompt.astype(f32)[None, :], (steps, rows)).reshape(-1, 1),
        (steps * rows, HDIM),
    )
    flat = lambda a: a.reshape(steps * rows, -1)
    mixed, mixed_sq, decoded, decoded_sq = fused(
        n,
        steps,
        query_in,
        key_in,
        value_in,
        tokens,
        bias,
        coef,
        masks,
        flat(step_query),
        flat(step_key),
        flat(step_value),
        step_weights,
        row_marks,
    )
    squares, step_squares = lax.psum(
        (mixed_sq[0], decoded_sq[0]), "head"
    )
    scale = lax.rsqrt(squares / (HEAD_COUNT * HDIM) + EPSILON)
    attn_out = (mixed * scale[:, None] * norm_gain[None, :]).astype(jnp.bfloat16)
    step_scale = lax.rsqrt(step_squares / (HEAD_COUNT * HDIM) + EPSILON)
    decode_out = (decoded * step_scale[:, None] * norm_gain[None, :]).astype(jnp.bfloat16)
    return (attn_out, decode_out.reshape(step_query.shape))


def solution(mesh):
    in_specs = (
        P("seq", "head"),
        P("seq", "head"),
        P("seq", "head"),
        P("seq", "head"),
        P("head"),
        P(),
        P(None, "seq", "head"),
        P(None, "seq", "head"),
        P(None, "seq", "head"),
        P(None, "seq", "head"),
        P("seq"),
    )
    out_specs = (P("seq", "head"), P(None, "seq", "head"))
    return jax.shard_map(
        functools.partial(local, mesh.shape["seq"]),
        mesh=mesh,
        in_specs=in_specs,
        out_specs=out_specs,
        check_vma=False,
    )
```

profile of v0, /device:TPU:0, one launch (start us, length us, event | category | flops | bytes accessed | tf_op | source)
XLA Modules:
  0.0 108.6 jit_solution(13579990990608442545)
XLA Ops:
  0.7 0.8 select_reduce_fusion.1
  1.4 0.7 fusion.5
  2.2 0.7 copy_bitcast_fusion
  2.9 0.6 reduce-window.6
  3.5 0.2 slice_reduce_fusion
  3.8 0.1 select_reduce_fusion
  3.9 0.1 convert_reduce_fusion
  4.0 0.1 exponential_select_fusion
  5.0 0.7 maximum_bitcast_fusion.token_ref
  5.7 0.7 broadcast_compare_fusion
  6.4 0.7 broadcast_in_dim.183.coef_ref
  8.5 0.7 broadcast_in_dim.184.mask_ref
  9.2 0.8 fusion.1.bias_ref
  10.0 1.0 fusion.2
  11.1 0.8 copy.34
  11.9 0.7 convert_element_type.50
  12.6 0.1 broadcast_in_dim.186
  12.7 0.7 broadcast_in_dim.187.row_ref
  13.3 83.6 %fused.1 = (f32[256,2048]{1,0:T(8,128)}, f32[8,256]{1,0:T(8,128)}, f32[64,2048]{1,0:T(8,128)}, f32[8,64]{1,0:T(8,128)}) custom-call(bf16[256,2048]{1,0:T(8,128)(2,1)} %query_ref.1, bf16[256,2048]{1,0:T(8,128)(2,1)} %key_ref.1, bf16[256,2048]{1,0:T(8,128)(2,1)} %value_ref.1, f32[16,8,256]{2,1,0:T(8,128)} %maximum_bitcast_fusion.token_ref, ...), custom_call_target="tpu_custom_call" | custom-call | tf_op jit(solution)/shard_map/fused/pallas_call | solution.py:422
  96.9 0.7 slice.14
  97.6 0.7 slice_bitcast_fusion
  98.3 5.6 %all-reduce = (f32[256]{0:T(256)S(1)}, f32[64]{0:T(128)S(1)}) all-reduce(f32[256]{0:T(256)S(1)} %bitcast.43, f32[64]{0:T(128)S(1)} %slice_bitcast_fusion), channel_id=1, replica_groups=mesh['seq'=8,'head'=4] {'head'}, use_global_device_ids=true, to_apply=%region_8.9 | all-reduce | flops 320 | bytes 2560 | tf_op jit(solution)/shard_map/psum | solution.py:575
  104.0 1.9 %multiply_convert_fusion.1 = bf16[64,2048]{1,0:T(8,128)(2,1)} fusion(f32[64,2048]{1,0:T(8,128)} %get-tuple-element.8, f32[2048]{0:T(1024)S(1)} %copy-done.1, f32[64]{0:T(128)S(1)} %add_rsqrt_fusion.1), kind=kLoop, calls=%fused_computation.1 | loop fusion | flops 393216 | bytes 794880 | tf_op jit(solution)/shard_map/convert_element_type | solution.py:581
  105.8 2.8 %multiply_convert_fusion = bf16[256,2048]{1,0:T(8,128)(2,1)} fusion(f32[256,2048]{1,0:T(8,128)} %get-tuple-element.6, f32[2048]{0:T(1024)S(1)} %copy-done.1, f32[256]{0:T(256)S(1)} %add_rsqrt_fusion), kind=kLoop, calls=%fused_computation | loop fusion | flops 1572864 | bytes 3154944 | tf_op jit(solution)/shard_map/convert_element_type | solution.py:579
  (24 shorter events, 0.6 us)
Async XLA Ops:
  0.6 9.4 %copy-start = (f32[4,16,16]{2,1,0:T(8,128)S(1)}, f32[4,16,16]{2,1,0:T(8,128)}, u32[]{:S(2)}) copy-start(f32[4,16,16]{2,1,0:T(8,128)} %param.21) | copy-start | bytes 12292
  13.3 90.6 %copy-start.1 = (f32[2048]{0:T(1024)S(1)}, f32[2048]{0:T(1024)}, u32[]{:S(2)}) copy-start(f32[2048]{0:T(1024)} %param.16) | copy-start | bytes 24580
where the time goes:
time: 109 us
  Pallas kernels  83.6 us (77%)
  other arithmetic  10.3 us (9%)
  blocking collectives  5.63 us (5%)
  local copies, waits for them, and re-layouts  5.37 us (5%)
  between operations  2.76 us (3%)
    pallas_call x1, Pallas kernels, fused(): pl.pallas_call(functools.partial(fused_kernel, n, steps), out_shape=(jax....  83.6 us
    psum x1, blocking collectives, local(): squares, step_squares = lax.psum((mixed_sq[0], decoded_sq[0]), 'head')  5.63 us
    convert_element_type x1, other arithmetic, local(): (mixed * scale[:, None] * norm_gain[None, :]).astype(jnp.bfloat16)  2.8 us

commit v1 on v0

v1 whole, which is shorter than its diff:
```python
import functools

import jax
import jax.numpy as jnp
from jax import lax
from jax.experimental import pallas as pl
from jax.experimental.pallas import tpu as pltpu
from jax.sharding import PartitionSpec as P

HDIM = 128
PROMPTS = 4
PAIR = 2
LAG = 3
AHEAD = 3
CUM_ROW = 4
CARRIED_ROW = 5

EPSILON = 1e-06
MESH = pl.DeviceIdType.MESH


def fused_kernel(
    n,
    n_head,
    steps,
    parts,
    fwd,
    bwd,
    lens_ref,
    prompt_ref,
    query_ref,
    key_ref,
    value_ref,
    decay_ref,
    gain_ref,
    sq_ref,
    sk_ref,
    sv_ref,
    sd_ref,
    attn_ref,
    out_ref,
    token_s,
    bias_s,
    weight_s,
    coef_s,
    coef_recv,
    row_s,
    row_recv,
    mixed_s,
    dec_s,
    own_part,
    x_send,
    x_recv,
    q_send,
    q_recv,
    f_recv,
    f_send,
    b_recv,
    b_send,
    pair_part,
    low_part,
    t_recv,
    t_send,
    e_mine,
    acc_sq,
    acc_dsq,
    acc_own,
    e_send,
    e_recv,
    r_send,
    r_recv,
    n_send,
    n_recv,
    d_send,
    d_recv,
    xs_sem,
    xr_sem,
    cs_sem,
    cr_sem,
    qs_sem,
    qr_sem,
    ws_sem,
    wr_sem,
    fs_sem,
    fr_sem,
    bs_sem,
    br_sem,
    ts_sem,
    tr_sem,
    es_sem,
    er_sem,
    rs_sem,
    rr_sem,
    ns_sem,
    nr_sem,
    ds_sem,
    dr_sem,
):
    f32, bf16, i32 = jnp.float32, jnp.bfloat16, jnp.int32
    me = lax.axis_index("seq")
    hd = lax.axis_index("head")
    side = lax.rem(me, PAIR)
    rank = lax.div(me, PAIR)
    ranks = n // PAIR
    partner = me + 1 - 2 * side
    half = own_part.shape[0]
    heads = PAIR * half
    tok, width = query_ref.shape
    slots = PROMPTS
    units = half * slots
    rows = sq_ref.shape[0] // steps
    mine = side * half
    theirs = (1 - side) * half
    is_first = rank == 0
    is_last = rank == ranks - 1
    low = side == 0
    ahead = lax.rem(me + PAIR, n)
    behind = lax.rem(me + n - PAIR, n)

    def copy(src, dst, send, recv, to):
        return pltpu.make_async_remote_copy(
            src_ref=src,
            dst_ref=dst,
            send_sem=send,
            recv_sem=recv,
            device_id=to,
            device_id_type=MESH,
        )

    def x_copy(j, k):
        i = j * parts + k
        return copy(
            x_send.at[j, k], x_recv.at[j, k], xs_sem.at[i], xr_sem.at[i], {"seq": partner}
        )

    def f_copy(j, p):
        i = j * slots + p
        return copy(f_send.at[j, p], f_recv.at[j, p], fs_sem.at[i], fr_sem.at[i], {"seq": ahead})

    def b_copy(j, p):
        i = j * slots + p
        return copy(b_send.at[j, p], b_recv.at[j, p], bs_sem.at[i], br_sem.at[i], {"seq": behind})

    def q_copy(j):
        return copy(q_send.at[j], q_recv.at[j], qs_sem.at[j], qr_sem.at[j], {"seq": partner})

    def e_copy(j):
        return copy(e_send.at[j], e_recv.at[j], es_sem.at[j], er_sem.at[j], {"seq": partner})

    def r_copy(j):
        return copy(r_send.at[j], r_recv.at[j], rs_sem.at[j], rr_sem.at[j], {"seq": partner})

    def peer(k):
        return {"head": lax.rem(hd + k, n_head)}

    def n_copy(k):
        return copy(n_send, n_recv.at[k - 1], ns_sem.at[k - 1], nr_sem.at[k - 1], peer(k))

    def d_copy(k):
        return copy(d_send, d_recv.at[k - 1], ds_sem.at[k - 1], dr_sem.at[k - 1], peer(k))

    coef_copy = copy(coef_s.at[1 - side], coef_recv, cs_sem, cr_sem, {"seq": partner})
    row_copy = copy(row_s, row_recv, ws_sem, wr_sem, {"seq": partner})
    t_copy = copy(t_send, t_recv, ts_sem, tr_sem, {"seq": behind})

    def lanes(h):
        return pl.ds(pl.multiple_of(h * HDIM, HDIM), HDIM)

    barrier = pltpu.get_barrier_semaphore()

    def greet(to):
        pl.semaphore_signal(barrier, inc=1, device_id=to, device_id_type=MESH)

    greet({"seq": partner})
    for k in range(1, n_head):
        greet(peer(k))

    @pl.when(jnp.logical_not(is_last))
    def _():
        greet({"seq": ahead})

    @pl.when(jnp.logical_not(is_first))
    def _():
        greet({"seq": behind})

    ends = []
    for p in range(slots):
        ends.append(lens_ref[p] + (ends[-1] if p else 0))
    begins = [ends[p] - lens_ref[p] for p in range(slots)]

    def number(flag):
        return jnp.where(flag, 1, 0).astype(i32)

    def unity(flag):
        return jnp.where(flag, 1.0, 0.0).astype(f32)

    def seg_of(token):
        total = number(token >= ends[0])
        for p in range(1, slots):
            total = total + number(token >= ends[p])
        return total

    def seg_before(token):
        return jnp.where(token > 0, seg_of(token - 1), -1)

    first = me * tok
    pair_first = rank * (PAIR * tok)
    base = seg_of(first)
    base_low = seg_of(pair_first)
    base_high = seg_of(pair_first + tok)
    front_low = seg_before(pair_first)
    front_high = seg_before(pair_first + tok)

    sub = lax.broadcasted_iota(i32, (tok, tok), 0)
    lane = lax.broadcasted_iota(i32, (tok, tok), 1)
    cum = jnp.dot(
        decay_ref[...],
        jnp.where(sub <= lane, 1.0, 0.0).astype(f32),
        precision=lax.Precision.HIGHEST,
        preferred_element_type=f32,
    )
    place = lax.broadcasted_iota(i32, (heads, tok), 1)
    segs = seg_of(place + first)
    goal = jnp.zeros_like(cum)
    for p in range(slots):
        last = jnp.clip(ends[p] - first, 1, tok) - 1
        reached = jnp.sum(jnp.where(place == last, cum, 0.0), axis=1, keepdims=True)
        goal = jnp.where(segs == p, reached, goal)
        grown = jnp.where(begins[p] < first, jnp.exp(reached), 0.0)
        coef = jnp.where(ends[p] <= first, 1.0, grown)
        coef = jnp.broadcast_to(coef, (heads, HDIM))
        for s in range(PAIR):
            coef_s[s, p] = coef[s * half : (s + 1) * half]
    keep = jnp.exp(goal - cum)
    carried = jnp.where(segs == seg_before(first), jnp.exp(cum), 0.0)
    keeps = [jnp.where(segs == base + k, keep, 0.0) for k in range(parts)]
    token_s[...] = jnp.zeros_like(token_s)
    for h in range(heads):
        at = slice(h, h + 1)
        for k in range(parts):
            token_s[h, k : k + 1, :] = keeps[k][at]
        token_s[h, CUM_ROW : CUM_ROW + 1, :] = cum[at]
        token_s[h, CARRIED_ROW : CARRIED_ROW + 1, :] = carried[at]

    def make_parts(h, j, into):
        key = key_ref[:, lanes(h)].astype(f32)
        value = value_ref[:, lanes(h)]
        cols = jnp.transpose(token_s[h])
        for k in range(parts):
            keyed = (key * cols[:, k : k + 1]).astype(bf16)
            into[j, k] = lax.dot_general(
                keyed, value, (((0,), (0,)), ((), ())), preferred_element_type=f32
            )

    def within(h):
        query = query_ref[:, lanes(h)]
        scores = lax.dot_general(
            query, key_ref[:, lanes(h)], (((1,), (1,)), ((), ())), preferred_element_type=f32
        )
        cols = jnp.transpose(token_s[h])
        column = cols[:, CUM_ROW : CUM_ROW + 1]
        spread = column - token_s[h, CUM_ROW : CUM_ROW + 1, :] + bias_s[...]
        weights = (scores * jnp.exp(spread)).astype(bf16)
        mixed_s[:, lanes(h)] = jnp.dot(
            weights, value_ref[:, lanes(h)], preferred_element_type=f32
        )

    def across(h, entry):
        column = jnp.transpose(token_s[h])[:, CARRIED_ROW : CARRIED_ROW + 1]
        outer = jnp.dot(query_ref[:, lanes(h)], entry.astype(bf16), preferred_element_type=f32)
        mixed = mixed_s[:, lanes(h)] + outer * column
        mixed_s[:, lanes(h)] = mixed
        acc_sq[...] += mixed * mixed

    pick = lax.broadcasted_iota(i32, (rows, heads), 1)

    def weight_col(i, h):
        return jnp.sum(jnp.where(pick == h, weight_s[i], 0.0), axis=1, keepdims=True)

    def own_steps(h):
        query = sq_ref[:, lanes(h)].astype(f32)
        key = sk_ref[:, lanes(h)].astype(f32)
        value = sv_ref[:, lanes(h)].astype(f32)
        cut = lambda a, i: a[i * rows : (i + 1) * rows]
        spot = steps
        for i in range(steps):
            total = None
            for j in range(i + 1):
                dot = jnp.sum(cut(query, i) * cut(key, j), axis=1, keepdims=True)
                if j < i:
                    dot = dot * weight_col(spot, h)
                    spot += 1
                term = dot * cut(value, j)
                total = term if j == 0 else total + term
            dec_s[i * rows : (i + 1) * rows, lanes(h)] = total

    def from_state(h, product):
        for i in range(steps):
            at = slice(i * rows, (i + 1) * rows)
            out = dec_s[at, lanes(h)] + weight_col(i, h) * product[at]
            dec_s[at, lanes(h)] = out
            acc_dsq[at] += out * out

    def send_parts(j):
        make_parts(theirs + j, j, x_send)
        for k in range(parts):
            x_copy(j, k).start()

    make_parts(theirs, 0, x_send)
    pl.semaphore_wait(
        barrier, n_head + jnp.where(is_first, 0, 1) + jnp.where(is_last, 0, 1)
    )
    coef_copy.start()
    for k in range(parts):
        x_copy(0, k).start()
    for j in range(1, AHEAD):
        send_parts(j)
    make_parts(mine, 0, own_part)

    column = lax.broadcasted_iota(i32, (rows, HDIM), 0)
    marks = jnp.zeros((rows, HDIM), f32)
    for r in range(rows):
        marks = jnp.where(column == r, prompt_ref[r].astype(f32), marks)
    row_s[...] = marks
    row_copy.start()
    tops = jnp.broadcast_to(segs[0:1].astype(f32), (8, tok))
    linked = (sub >= lane) & (jnp.transpose(tops)[:, 0:1] == tops[0:1])
    bias_s[...] = jnp.where(linked, 0.0, -jnp.inf)
    totals = []
    for i in range(steps):
        totals.append(sd_ref[i] + totals[-1] if i else sd_ref[i])
    spot = steps
    for i in range(steps):
        weight_s[i] = jnp.exp(totals[i])
        for j in range(i):
            weight_s[spot] = jnp.exp(totals[i] - totals[j])
            spot += 1
    acc_sq[...] = jnp.zeros_like(acc_sq)
    acc_dsq[...] = jnp.zeros_like(acc_dsq)
    if fwd < slots:
        f_recv[:, fwd:] = jnp.zeros((half, slots - fwd, HDIM, HDIM), f32)
    if bwd > 0:
        b_recv[:, :bwd] = jnp.zeros((half, bwd, HDIM, HDIM), f32)

    @pl.when(is_first)
    def _():
        f_recv[:, :fwd] = jnp.zeros((half, fwd, HDIM, HDIM), f32)

    @pl.when(is_last)
    def _():
        b_recv[:, bwd:] = jnp.zeros((half, slots - bwd, HDIM, HDIM), f32)
        t_recv[...] = jnp.ones_like(t_recv)

    coef_copy.wait()
    row_copy.wait()

    lag_f = rank * LAG
    lag_b = (ranks - 1 - rank) * LAG
    lag_d = jnp.maximum(lag_f, lag_b)

    def relay_decay():
        @pl.when(jnp.logical_not(is_last))
        def _():
            t_copy.wait_recv()

        @pl.when(jnp.logical_not(is_first))
        def _():
            t_send[...] = t_recv[...] * coef_recv[...] * coef_s[side]
            t_copy.start()

    def rows_of(j, p):
        c_own = coef_s[side, p, pl.ds(j, 1), :]
        c_other = coef_recv[p, pl.ds(j, 1), :]
        return jnp.where(low, c_own, c_other), jnp.where(low, c_other, c_own)

    def combine(j, p):
        @pl.when(p == 0)
        def _():
            for k in range(parts):
                x_copy(j, k).wait_recv()

        base_own = jnp.where(low, base_low, base_high)
        base_other = jnp.where(low, base_high, base_low)
        own = None
        other = None
        for k in range(parts):
            a = unity(base_own + k == p) * own_part[j, k]
            b = unity(base_other + k == p) * x_recv[j, k]
            own = a if k == 0 else own + a
            other = b if k == 0 else other + b
        c_low, c_high = rows_of(j, p)
        at_low = jnp.where(low, own, other)
        low_part[j, p] = at_low
        pair_part[j, p] = c_high * at_low + jnp.where(low, other, own)

    def forward(j, p):
        @pl.when(jnp.logical_not(is_first) & (p < fwd))
        def _():
            f_copy(j, p).wait_recv()

        c_low, c_high = rows_of(j, p)
        came = f_recv[j, p]
        middle = c_low * came
        f_send[j, p] = c_high * middle + pair_part[j, p]

        @pl.when(jnp.logical_not(is_last) & (p < fwd))
        def _():
            f_copy(j, p).start()

        at_low = came * unity(front_low == p)
        at_high = (middle + low_part[j, p]) * unity(front_high == p)
        to_mine = jnp.where(low, at_low, at_high)
        to_theirs = jnp.where(low, at_high, at_low)

        @pl.when(p == 0)
        def _():
            e_mine[j] = to_mine
            e_send[j] = to_theirs

        @pl.when(p > 0)
        def _():
            e_mine[j] += to_mine
            e_send[j] += to_theirs

        @pl.when(p == slots - 1)
        def _():
            e_copy(j).start()

    def backward(j, p):
        @pl.when(jnp.logical_not(is_last) & (p >= bwd))
        def _():
            b_copy(j, p).wait_recv()

        @pl.when(jnp.logical_not(is_first) & (p >= bwd))
        def _():
            t_row = t_recv[p, pl.ds(j, 1), :]
            b_send[j, p] = b_recv[j, p] + t_row * pair_part[j, p]
            b_copy(j, p).start()

    def decode(j, p):
        @pl.when(p == 0)
        def _():
            q_copy(j).wait_recv()

        t_row = t_recv[p, pl.ds(j, 1), :]
        final = (t_row * f_send[j, p] + b_recv[j, p]).astype(bf16)
        got_own = jnp.dot(sq_ref[:, lanes(mine + j)], final, preferred_element_type=f32)
        got_other = jnp.dot(q_recv[j].astype(bf16), final, preferred_element_type=f32)
        slot = p.astype(f32)
        spread = lambda a: jnp.concatenate([a] * steps, axis=0)
        got_own = jnp.where(spread(row_s[...]) == slot, got_own, 0.0)
        got_other = jnp.where(spread(row_recv[...]) == slot, got_other, 0.0)

        @pl.when(p == 0)
        def _():
            acc_own[...] = got_own
            r_send[j] = got_other

        @pl.when(p > 0)
        def _():
            acc_own[...] += got_own
            r_send[j] += got_other

        @pl.when(p == slots - 1)
        def _():
            r_copy(j).start()
            from_state(mine + j, acc_own[...])

    def split(t):
        return lax.div(t, slots), lax.rem(t, slots)

    @pl.loop(0, units + (ranks - 1) * LAG)
    def _(t):
        j, p = split(t)

        @pl.when(t < units)
        def _():
            combine(j, p)

        @pl.when(t == lag_b)
        def _():
            relay_decay()

        @pl.when((t >= lag_f) & (t < units + lag_f))
        def _():
            forward(*split(t - lag_f))

        @pl.when((t >= lag_b) & (t < units + lag_b))
        def _():
            backward(*split(t - lag_b))

        @pl.when((t < units) & (p == 0))
        def _():
            q_send[j] = sq_ref[:, lanes(theirs + j)].astype(f32)
            q_copy(j).start()

            @pl.when(j < half - AHEAD)
            def _():
                send_parts(j + AHEAD)

        @pl.when((t < units) & (p == 1))
        def _():
            own_steps(mine + j)
            within(mine + j)

        @pl.when((t < units) & (p == 2))
        def _():
            own_steps(theirs + j)
            within(theirs + j)

            @pl.when(j < half - 1)
            def _():
                make_parts(mine + j + 1, j + 1, own_part)

        @pl.when((t >= lag_d) & (t < units + lag_d))
        def _():
            decode(*split(t - lag_d))

        @pl.when((t >= lag_f) & (t < units + lag_f))
        def _():
            jf, pf = split(t - lag_f)

            @pl.when(pf == slots - 1)
            def _():
                across(mine + jf, e_mine[jf])

    @pl.loop(0, half)
    def _(j):
        e_copy(j).wait()
        across(theirs + j, e_recv[j])

    def row_sums(acc):
        return lax.dot_general(
            jnp.ones((8, HDIM), f32),
            acc[...],
            (((1,), (1,)), ((), ())),
            precision=lax.Precision.HIGHEST,
            preferred_element_type=f32,
        )

    def scale_of(total):
        scale = lax.rsqrt(total / (n_head * width) + EPSILON)
        return jnp.transpose(scale)[:, 0:1]

    n_send[...] = row_sums(acc_sq)
    for k in range(1, n_head):
        n_copy(k).start()

    @pl.loop(0, half)
    def _(j):
        r_copy(j).wait()
        from_state(theirs + j, r_recv[j])

    d_send[...] = row_sums(acc_dsq)
    for k in range(1, n_head):
        d_copy(k).start()

    total = n_send[...]
    for k in range(1, n_head):
        n_copy(k).wait()
        total = total + n_recv[k - 1]
    scale = jnp.broadcast_to(scale_of(total), (tok, HDIM))

    @pl.loop(0, heads)
    def _(h):
        at = lanes(h)
        attn_ref[:, at] = (mixed_s[:, at] * scale * gain_ref[:, at]).astype(bf16)

    total = d_send[...]
    for k in range(1, n_head):
        d_copy(k).wait()
        total = total + d_recv[k - 1]
    dec_scale = scale_of(total)
    out_ref[...] = (dec_s[...] * dec_scale * gain_ref[...]).astype(bf16)

    @pl.loop(0, half)
    def _(j):
        q_copy(j).wait_send()
        for k in range(parts):
            x_copy(j, k).wait_send()

        for p in range(fwd):

            @pl.when(jnp.logical_not(is_last))
            def _():
                f_copy(j, p).wait_send()

        for p in range(bwd, slots):

            @pl.when(jnp.logical_not(is_first))
            def _():
                b_copy(j, p).wait_send()

    @pl.when(jnp.logical_not(is_first))
    def _():
        t_copy.wait_send()


def fused(n, n_head, steps, variant, collective, *operands):
    parts, fwd, bwd = variant
    query, decay, step, step_decay = operands[2], operands[5], operands[7], operands[10]
    tok, width = query.shape
    heads = decay.shape[0]
    half = heads // PAIR
    vectors = step.shape[0]
    rows = vectors // steps
    slots = PROMPTS
    f32, bf16 = jnp.float32, jnp.bfloat16
    vmem = pl.BlockSpec(memory_space=pltpu.VMEM)
    smem = pl.BlockSpec(memory_space=pltpu.SMEM)
    dma = pltpu.SemaphoreType.DMA
    buffer = lambda *shape: pltpu.VMEM(shape, f32)
    states = buffer(half, slots, HDIM, HDIM)
    pieces = buffer(half, parts, HDIM, HDIM)
    decays = buffer(slots, half, HDIM)
    entries = buffer(half, HDIM, HDIM)
    products = buffer(half, vectors, HDIM)
    return pl.pallas_call(
        functools.partial(fused_kernel, n, n_head, steps, parts, fwd, bwd),
        out_shape=(
            jax.ShapeDtypeStruct((tok, width), bf16),
            jax.ShapeDtypeStruct((vectors, width), bf16),
        ),
        in_specs=[smem] * 2 + [vmem] * (len(operands) - 2),
        out_specs=(vmem,) * 2,
        scratch_shapes=[
            buffer(heads, 8, tok),
            buffer(tok, tok),
            buffer(steps * (steps + 1) // 2, rows, heads),
            buffer(PAIR, slots, half, HDIM),
            decays,
            buffer(rows, HDIM),
            buffer(rows, HDIM),
            buffer(tok, width),
            buffer(vectors, width),
            pieces,
            pieces,
            pieces,
            products,
            products,
            states,
            states,
            states,
            states,
            states,
            states,
            decays,
            decays,
            entries,
            buffer(tok, HDIM),
            buffer(vectors, HDIM),
            buffer(vectors, HDIM),
            entries,
            entries,
            products,
            products,
            buffer(8, tok),
            buffer(n_head - 1, 8, tok),
            buffer(8, vectors),
            buffer(n_head - 1, 8, vectors),
            dma((half * parts,)),
            dma((half * parts,)),
            dma,
            dma,
            dma((half,)),
            dma((half,)),
            dma,
            dma,
            dma((half * slots,)),
            dma((half * slots,)),
            dma((half * slots,)),
            dma((half * slots,)),
            dma,
            dma,
            dma((half,)),
            dma((half,)),
            dma((half,)),
            dma((half,)),
            dma((n_head - 1,)),
            dma((n_head - 1,)),
            dma((n_head - 1,)),
            dma((n_head - 1,)),
        ],
        compiler_params=pltpu.CompilerParams(
            collective_id=collective, has_side_effects=True, vmem_limit_bytes=56 * 1024 * 1024
        ),
        name="fused",
    )(*operands)


def local(
    n,
    n_head,
    query_in,
    key_in,
    value_in,
    log_decay,
    norm_gain,
    prompt_lengths,
    step_query,
    step_key,
    step_value,
    step_decay,
    row_prompt,
):
    steps, rows = step_query.shape[:2]
    flat = lambda a: a.reshape(steps * rows, -1)
    attn_out, decode_out = fused(
        n,
        n_head,
        steps,
        (PROMPTS, PROMPTS, 0),
        0,
        prompt_lengths,
        row_prompt,
        query_in,
        key_in,
        value_in,
        log_decay.T,
        norm_gain[None, :],
        flat(step_query),
        flat(step_key),
        flat(step_value),
        step_decay,
    )
    return (attn_out, decode_out.reshape(step_query.shape))


def solution(mesh):
    in_specs = (
        P("seq", "head"),
        P("seq", "head"),
        P("seq", "head"),
        P("seq", "head"),
        P("head"),
        P(),
        P(None, "seq", "head"),
        P(None, "seq", "head"),
        P(None, "seq", "head"),
        P(None, "seq", "head"),
        P("seq"),
    )
    out_specs = (P("seq", "head"), P(None, "seq", "head"))
    return jax.shard_map(
        functools.partial(local, mesh.shape["seq"], mesh.shape["head"]),
        mesh=mesh,
        in_specs=in_specs,
        out_specs=out_specs,
        check_vma=False,
    )
```

time: 109 us -> 97.1 us (0.89)
  other arithmetic: 10.3 us -> 0 us
  Pallas kernels: 83.6 us -> 93.3 us
  blocking collectives: 5.63 us -> 0 us
  local copies, waits for them, and re-layouts: 5.37 us -> 3.05 us
  between operations: 2.76 us -> 0.65 us
    pallas_call x1, Pallas kernels: 83.6 us -> 93.3 us  [fused(): pl.pallas_call(functools.partial(fused_kernel, n, n_head, steps, parts, f...]
    psum x1 -> x0, blocking collectives: 5.63 us -> none  [local(): squares, step_squares = lax.psum((mixed_sq[0], decoded_sq[0]), 'head')]
    convert_element_type x5 -> x0, other arithmetic: 5.41 us -> none  [the longest x1 2.8 us: local(): (mixed * scale[:, None] * norm_gain[None, :]).astype(jnp.bfloat16)]
    unnamed x4, local copies, waits for them, and re-layouts: 0.01 us -> 3.05 us
    broadcast_in_dim x8 -> x0, local copies, waits for them, and re-layouts: 2.16 us -> none  [the longest x2 0.77 us: local(): jnp.broadcast_to(jnp.broadcast_to(row_prompt.astype(f32)[None, :], (steps...]
    reduce_sum x4 -> x0, other arithmetic: 1.67 us -> none  [the longest x2 0.8 us: segment_ids(): jnp.sum((positions[:, None] >= boundary[None, :]).astype(jnp.int32), axis=1)]
where the time goes in v1:
time: 97.1 us; the launch traced here: 97 us
  Pallas kernels  93.3 us (96%)
  local copies, waits for them, and re-layouts  3.05 us (3%)
    pallas_call x1, Pallas kernels, fused(): pl.pallas_call(functools.partial(fused_kernel, n, n_head, steps, parts, f...  93.3 us
    unnamed x4, local copies, waits for them, and re-layouts  3.05 us

profile of v1, /device:TPU:0, one launch (start us, length us, event | category | flops | bytes accessed | tf_op | source)
XLA Modules:
  0.0 97.0 jit_solution(146164002763672821)
XLA Ops:
  0.6 93.3 %fused.1 = (bf16[256,2048]{1,0:T(8,128)(2,1)}, bf16[64,2048]{1,0:T(8,128)(2,1)}) custom-call(s32[4]{0:T(128)} %lens_ref.1, s32[16]{0:T(128)} %prompt_ref.1, bf16[256,2048]{1,0:T(8,128)(2,1)} %query_ref.1, bf16[256,2048]{1,0:T(8,128)(2,1)} %key_ref.1, bf16[256,2048]{1,0:T(8,128)(2,1)} %value_ref.1, f32[16,256]{1,0:T(8,128)} %bitcast.10, f32[1,2048]{1,0:T(1,128)} %bitcast.11, ...), custom_call_target="tpu_custom_call" | custom-call | tf_op jit(solution)/shard_map/fused/pallas_call | solution.py:618
  93.9 0.0 copy-start
  93.9 2.3 %copy.15 = bf16[256,2048]{1,0:T(8,128)(2,1)} copy(bf16[256,2048]{1,0:T(8,128)(2,1)} %get-tuple-element.8) | data formatting | bytes 2097152
  96.3 0.0 copy-done
  96.3 0.7 copy.16
Async XLA Ops:
  93.9 2.4 %copy-start = (bf16[64,2048]{1,0:T(8,128)(2,1)S(1)}, bf16[64,2048]{1,0:T(8,128)(2,1)}, u32[]{:S(2)}) copy-start(bf16[64,2048]{1,0:T(8,128)(2,1)} %get-tuple-element.5) | copy-start | bytes 786436
